TPU v7x, 32 devices: a whole 2x2x4 slice. The times are simulated.
32 devices in a mesh: slab: 2 (over x), grp: 16 (over z, y, core).
Axes of the slice: x: 2, y: 2, z: 4, core: 2. Of those that a mesh axis runs over, the one named last changes fastest.
Arguments:
- blocks: bfloat16 [128, 9, 256, 256], P(('slab', 'grp')), may hold values from -0.75 to 0.75
- diag_shift: float32 [32768], P(('slab', 'grp')), may hold values from 1 to 16
- offsets: int32 [128, 2], P(('slab', 'grp')), may hold values from 0 to 4
Outputs:
- factors: bfloat16 [128, 9, 256, 256], P(('slab', 'grp'))
Inputs may be any that keep to these rules, and one draw needn't show every extreme that they name: offsets[i, 0] bounds from above the pattern's blocks left of the diagonal block of block row i and offsets[i, 1] those right of it; blocks that would lie outside the matrix are not in the pattern.
All inputs are finite; a program needn't handle non-finite values.
Results may differ from a plain program's by a relative error of at most 0.001.
Values may be sent and summed in bfloat16 or wider, within the bound.
A program may use at most 256 MiB of HBM per device.

v0:
```python
import functools

import jax
import jax.numpy as jnp
from jax import lax
from jax.experimental import pallas as pl
from jax.experimental.pallas import tpu as pltpu
from jax.sharding import PartitionSpec as P

MESH = pl.DeviceIdType.MESH
F32 = jnp.float32
BF16 = jnp.bfloat16

DIAG, SHIFT, UPPER, LOWER, SENT = 0, 1, 2, 8, 8


def band_pattern(global_rows, offsets, band_count, all_rows):
    band_reach = (band_count - 1) // 2
    relative = jnp.arange(band_count, dtype=jnp.int32) - band_reach
    lower_count = offsets[:, 0:1]
    upper_count = offsets[:, 1:2]
    target = global_rows[:, None] + relative[None, :]
    left_side = (relative < 0) & (-relative <= lower_count) & (target >= 0)
    right_side = (relative > 0) & (relative <= upper_count) & (target < all_rows)
    return (relative == 0) | left_side | right_side


def kernel(
    slabs, groups, reach,
    blocks, aux, out,
    blk, aux_own, aux_prev, aux_next, scale, a, w1, w2, low2, h1, f2,
    load_sem, aux_load_sem, out_sem, aux_send, aux_recv, send1, recv1, send2, recv2,
):
    rows, band, size, _ = blk.shape
    slab, grp = lax.axis_index("slab"), lax.axis_index("grp")
    here = slab * groups + grp
    has_prev = here > 0
    has_next = here < slabs * groups - 1
    after = lax.rem(here + 1, slabs * groups)
    before = lax.rem(here + slabs * groups - 1, slabs * groups)
    nxt = (lax.div(after, groups), lax.rem(after, groups))
    prv = (lax.div(before, groups), lax.rem(before, groups))
    inner = grp < groups - 1
    edge = jnp.logical_and(grp == groups - 1, has_next)

    def copy1(j, src):
        return pltpu.make_async_remote_copy(
            src_ref=src, dst_ref=h1.at[j], send_sem=send1.at[j], recv_sem=recv1.at[j],
            device_id=nxt, device_id_type=MESH,
        )

    def copy2(j, src):
        return pltpu.make_async_remote_copy(
            src_ref=src, dst_ref=w2.at[j], send_sem=send2.at[j], recv_sem=recv2.at[j],
            device_id=nxt, device_id_type=MESH,
        )

    def load(j):
        return pltpu.make_async_copy(blocks.at[j], blk.at[j], load_sem.at[j])

    def raw_upper(j):
        return blocks.at[j, pl.ds(reach, reach + 1)]

    aux_head = aux.at[:, pl.ds(0, SENT)]
    to_next = pltpu.make_async_remote_copy(
        src_ref=aux_head, dst_ref=aux_prev, send_sem=aux_send.at[0], recv_sem=aux_recv.at[0],
        device_id=nxt, device_id_type=MESH,
    )
    to_prev = pltpu.make_async_remote_copy(
        src_ref=aux_head, dst_ref=aux_next, send_sem=aux_send.at[1], recv_sem=aux_recv.at[1],
        device_id=prv, device_id_type=MESH,
    )
    aux_load = pltpu.make_async_copy(aux, aux_own, aux_load_sem.at[0])

    aux_load.start()
    for j in range(rows):
        load(j).start()

    barrier = pltpu.get_barrier_semaphore()

    @pl.when(has_prev)
    def _():
        pl.semaphore_signal(barrier, inc=1, device_id=prv, device_id_type=MESH)

    @pl.when(has_next)
    def _():
        pl.semaphore_signal(barrier, inc=1, device_id=nxt, device_id_type=MESH)

    pl.semaphore_wait(barrier, has_prev.astype(jnp.int32) + has_next.astype(jnp.int32))

    @pl.when(has_prev)
    def _():
        to_prev.start()

    @pl.when(has_next)
    def _():
        to_next.start()

    @pl.when(inner)
    def _():
        for j in reversed(range(rows)):
            copy1(j, raw_upper(j)).start()

    row_id = lax.broadcasted_iota(jnp.int32, (size, size), 0)
    col_id = lax.broadcasted_iota(jnp.int32, (size, size), 1)
    eye = row_id == col_id

    def scale_of(values):
        positive = values > 0
        return jnp.where(positive, 1.0 / jnp.sqrt(jnp.where(positive, values, 1.0)), 0.0)

    def as_column(row):
        return jnp.sum(jnp.where(eye, row, 0.0), axis=1, keepdims=True)

    @pl.when(jnp.logical_not(has_prev))
    def _():
        aux_prev[...] = jnp.zeros_like(aux_prev)
        for j in range(reach):
            for k in range(reach + 1):
                w1[j, k] = jnp.zeros((size, size), BF16)
                w2[j, k] = jnp.zeros((size, size), BF16)

    @pl.when(jnp.logical_not(has_next))
    def _():
        aux_next[...] = jnp.zeros_like(aux_next)

    aux_load.wait()

    @pl.when(has_prev)
    def _():
        to_next.wait_recv()

    @pl.when(has_next)
    def _():
        to_prev.wait_recv()

    for j in range(rows):
        scale[j] = scale_of(aux_prev[j, DIAG : DIAG + 1, :])
        scale[rows + j] = scale_of(aux_own[j, DIAG : DIAG + 1, :])
        scale[2 * rows + j] = scale_of(aux_next[j, DIAG : DIAG + 1, :])

    def mask_of(table, j, k):
        place = UPPER + k - reach if k >= reach else LOWER + k
        return table[j, place : place + 1, :] > 0.5

    def scaled_block(block, table, j, k, shift, left, right):
        value = block.astype(F32)
        if k == reach:
            value = value + jnp.where(eye, shift, 0.0)
        value = value * left * right
        return jnp.where(mask_of(table, j, k), value, 0.0).astype(BF16)

    def scale_own(j, carry):
        load(j).wait()
        left = as_column(scale[rows + j])
        shift = aux_own[j, SHIFT : SHIFT + 1, :]
        for k in range(band):
            value = scaled_block(blk[j, k], aux_own, j, k, shift, left, scale[j + k])
            a[j, k] = value
            if k >= reach:
                w1[reach + j, k - reach] = value
        return carry

    lax.fori_loop(0, rows, scale_own, 0)

    def update(j, low, w, put):
        def dot(x, y):
            return jnp.dot(x, y, preferred_element_type=F32)

        def partial(k):
            total = a[j, k].astype(F32)
            for m in range(1, reach + 1):
                s = k - reach + m
                if 1 <= s <= reach:
                    total = total - dot(low[j, reach - m], w[reach + j - m, s])
            return total

        def finish(k, value):
            put(k, jnp.where(mask_of(aux_own, j, k), value, 0.0).astype(BF16))

        own = w[reach + j, 0].astype(F32)
        below = row_id > col_id
        strict_low = jnp.where(below, own, 0.0).astype(BF16)
        for k in range(reach + 1, band):
            finish(k, partial(k) - dot(strict_low, w[reach + j, k - reach]))
        strict_up = jnp.where(row_id < col_id, own, 0.0).astype(BF16)
        rest = partial(reach) - dot(strict_low, strict_up)
        pivots = jnp.sum(jnp.where(eye, own, 0.0), axis=0, keepdims=True)
        finish(reach, jnp.where(below, rest / pivots, rest))
        for k in range(reach):
            m = reach - k
            pivot = w[reach + j - m, 0].astype(F32)
            strict = jnp.where(row_id < col_id, pivot, 0.0).astype(BF16)
            rest = partial(k) - dot(low[j, k], strict)
            pivots = jnp.sum(jnp.where(eye, pivot, 0.0), axis=0, keepdims=True)
            divisor = jnp.where(mask_of(aux_own, j, k), pivots, 1.0)
            finish(k, rest / divisor)

    def first_sweep(i, carry):
        j = rows - 1 - i

        @pl.when(has_prev)
        def _():
            copy1(j, w2.at[reach + j]).wait_recv()

        @pl.when(grp > 0)
        def _():
            left = as_column(scale[j])
            shift = aux_prev[j, SHIFT : SHIFT + 1, :]
            for k in range(reach + 1):
                w1[j, k] = scaled_block(
                    h1[j, k], aux_prev, j, reach + k, shift, left, scale[j + k]
                )

        @pl.when(jnp.logical_and(grp == 0, has_prev))
        def _():
            for k in range(reach + 1):
                w1[j, k] = h1[j, k]

        def put(k, value):
            if k >= reach:
                w2[reach + j, k - reach] = value
            else:
                low2[j, k] = value

        update(j, a, w1, put)

        @pl.when(inner)
        def _():
            copy2(j, w2.at[reach + j]).start()

        @pl.when(edge)
        def _():
            copy1(j, w2.at[reach + j]).start()

        return carry

    lax.fori_loop(0, rows, first_sweep, 0)

    def second_sweep(i, carry):
        j = rows - 1 - i

        @pl.when(has_prev)
        def _():
            copy2(j, w2.at[reach + j]).wait_recv()

        def put(k, value):
            f2[j, k] = value

        update(j, low2, w2, put)

        @pl.when(edge)
        def _():
            copy2(j, f2.at[j, pl.ds(reach, reach + 1)]).start()

        pltpu.make_async_copy(f2.at[j], out.at[j], out_sem.at[j]).start()
        return carry

    lax.fori_loop(0, rows, second_sweep, 0)

    for j in range(rows):
        pltpu.make_async_copy(f2.at[j], out.at[j], out_sem.at[j]).wait()

    @pl.when(has_next)
    def _():
        to_next.wait_send()
        for j in range(rows):
            copy1(j, w2.at[reach + j]).wait_send()
            copy2(j, w2.at[reach + j]).wait_send()

    @pl.when(has_prev)
    def _():
        to_prev.wait_send()


def per_device(blocks, diag_shift, offsets):
    rows, band, size, _ = blocks.shape
    reach = (band - 1) // 2
    assert rows == reach and reach <= 4
    slabs, groups = lax.axis_size("slab"), lax.axis_size("grp")
    first_row = (lax.axis_index("slab") * groups + lax.axis_index("grp")) * rows
    shift = diag_shift.reshape(rows, size)
    eye = jnp.eye(size, dtype=bool)
    diagonal = jnp.sum(jnp.where(eye[None], blocks[:, reach].astype(F32), 0.0), axis=1)
    present = band_pattern(
        first_row + jnp.arange(rows, dtype=jnp.int32), offsets, band, rows * slabs * groups
    ).astype(F32)
    marks = jnp.broadcast_to(present[:, :, None], (rows, band, size))
    pieces = [(shift + diagonal)[:, None], shift[:, None], marks[:, reach:]]
    pieces.append(jnp.zeros((rows, LOWER - UPPER - reach - 1, size), F32))
    pieces.append(marks[:, :reach])
    pieces.append(jnp.zeros((rows, 16 - LOWER - reach, size), F32))
    aux = jnp.concatenate(pieces, axis=1)

    block = (size, size)
    upper = (reach + 1,) + block
    dma = pltpu.SemaphoreType.DMA
    return pl.pallas_call(
        functools.partial(kernel, slabs, groups, reach),
        out_shape=jax.ShapeDtypeStruct(blocks.shape, BF16),
        in_specs=[pl.BlockSpec(memory_space=pl.ANY)] * 2,
        out_specs=pl.BlockSpec(memory_space=pl.ANY),
        scratch_shapes=[
            pltpu.VMEM(blocks.shape, BF16),
            pltpu.VMEM(aux.shape, F32),
            pltpu.VMEM((rows, SENT, size), F32),
            pltpu.VMEM((rows, SENT, size), F32),
            pltpu.VMEM((3 * rows, 1, size), F32),
            pltpu.VMEM(blocks.shape, BF16),
            pltpu.VMEM((reach + rows,) + upper, BF16),
            pltpu.VMEM((reach + rows,) + upper, BF16),
            pltpu.VMEM((rows, reach) + block, BF16),
            pltpu.VMEM((rows,) + upper, BF16),
            pltpu.VMEM(blocks.shape, BF16),
            dma((rows,)), dma((1,)), dma((rows,)), dma((2,)), dma((2,)),
            dma((rows,)), dma((rows,)), dma((rows,)), dma((rows,)),
        ],
        compiler_params=pltpu.CompilerParams(collective_id=0, has_side_effects=True),
    )(blocks, aux)


def solution(mesh):
    return jax.shard_map(
        per_device,
        mesh=mesh,
        in_specs=(
            P(("slab", "grp"), None, None, None),
            P(("slab", "grp")),
            P(("slab", "grp"), None),
        ),
        out_specs=P(("slab", "grp"), None, None, None),
        check_vma=False,
    )
```

profile of v0, /device:TPU:2, one launch (start us, length us, event | category | flops | bytes accessed | tf_op | source)
XLA Modules:
  0.0 84.3 jit_solution(6949549516597760685)
XLA Ops:
  0.0 0.8 slice_bitcast_fusion.1
  0.8 0.1 fusion.4
  0.9 0.1 slice.26
  0.9 0.1 broadcast_in_dim.39
  1.0 0.1 broadcast_in_dim.22
  1.1 1.2 %fusion = f32[4,256]{1,0:T(4,128)S(1)} fusion(bf16[4,9,256,256]{3,2,1,0:T(8,128)(2,1)} %blocks.1, pred[256,256]{1,0:T(8,128)(4,1)S(1)} %iota_compare_fusion), kind=kLoop, calls=%fused_computation.1 | loop fusion | flops 785408 | bytes 593920 | tf_op jit(solution)/shard_map/reduce_sum | solution.py:284
  2.3 0.7 reshape_add_fusion
  3.0 2.0 %concatenate.3.aux = f32[4,16,256]{2,1,0:T(8,128)} concatenate(f32[4,1,256]{2,1,0:T(1,128)S(1)} %reshape_add_fusion, f32[4,1,256]{2,1,0:T(1,128)} %bitcast.11, f32[4,5,256]{2,1,0:T(8,128)S(1)} %broadcast_in_dim.22, f32[4,1,256]{2,1,0:T(1,128)S(1)} %broadcast_in_dim.38, f32[4,4,256]{2,1,0:T(4,128)S(1)} %broadcast_in_dim.39, f32[4,4,256]{2,1,0:T(4,128)S(1)} %broadcast_in_dim.40), dimensions={1} | concatenate | bytes 131072 | tf_op jit(solution)/shard_map/concatenate | solution.py:293
  5.0 74.3 %shard_map.37 = bf16[4,9,256,256]{3,2,1,0:T(8,128)(2,1)} custom-call(bf16[4,9,256,256]{3,2,1,0:T(8,128)(2,1)} %blocks.1, f32[4,16,256]{2,1,0:T(8,128)} %concatenate.3.aux), custom_call_target="tpu_custom_call" | custom-call | tf_op jit(solution)/shard_map/pallas_call | solution.py:298
  79.3 5.0 %copy.5 = bf16[4,9,256,256]{3,2,1,0:T(8,128)(2,1)} copy(bf16[4,9,256,256]{3,2,1,0:T(8,128)(2,1)} %shard_map.37) | data formatting | bytes 9437184
  (7 shorter events, 0.1 us)
where the time goes:
time: 84.6 us; the launch traced here: 84.3 us
  Pallas kernels  74.3 us (88%)
  local copies, waits for them, and re-layouts  7.97 us (9%)
  other arithmetic  2.01 us (2%)
    pallas_call x1, Pallas kernels, per_device(): pl.pallas_call(functools.partial(kernel, slabs, groups, reach), out_shape...  74.3 us
    unnamed x1, local copies, waits for them, and re-layouts  5.03 us
    concatenate x1, local copies, waits for them, and re-layouts, per_device(): aux = jnp.concatenate(pieces, axis=1)  1.96 us

commit v1 on v0

--- a/solution.py
+++ b/solution.py
@@ -14,22 +14,11 @@
 DIAG, SHIFT, UPPER, LOWER, SENT = 0, 1, 2, 8, 8
 
 
-def band_pattern(global_rows, offsets, band_count, all_rows):
-    band_reach = (band_count - 1) // 2
-    relative = jnp.arange(band_count, dtype=jnp.int32) - band_reach
-    lower_count = offsets[:, 0:1]
-    upper_count = offsets[:, 1:2]
-    target = global_rows[:, None] + relative[None, :]
-    left_side = (relative < 0) & (-relative <= lower_count) & (target >= 0)
-    right_side = (relative > 0) & (relative <= upper_count) & (target < all_rows)
-    return (relative == 0) | left_side | right_side
-
-
 def kernel(
     slabs, groups, reach,
-    blocks, aux, out,
-    blk, aux_own, aux_prev, aux_next, scale, a, w1, w2, low2, h1, f2,
-    load_sem, aux_load_sem, out_sem, aux_send, aux_recv, send1, recv1, send2, recv2,
+    blocks, shifts, offsets, f2,
+    blk, shift_own, aux_own, aux_prev, aux_next, scale, a, w1, w2, low2, h1,
+    load_sem, aux_load_sem, aux_send, aux_recv, send1, recv1, send2, recv2,
 ):
     rows, band, size, _ = blk.shape
     slab, grp = lax.axis_index("slab"), lax.axis_index("grp")
@@ -43,25 +32,54 @@
     inner = grp < groups - 1
     edge = jnp.logical_and(grp == groups - 1, has_next)
 
+    half = size // 2
+
+    def pieces(src, dst, send, recv):
+        top, low = pl.ds(0, half), pl.ds(half, half)
+        cuts = ((0, top), (0, low, low), (pl.ds(1, reach),))
+        return [
+            pltpu.make_async_remote_copy(
+                src_ref=src.at[cut], dst_ref=dst.at[cut],
+                send_sem=send.at[n], recv_sem=recv.at[n],
+                device_id=nxt, device_id_type=MESH,
+            )
+            for n, cut in enumerate(cuts)
+        ]
+
     def copy1(j, src):
-        return pltpu.make_async_remote_copy(
-            src_ref=src, dst_ref=h1.at[j], send_sem=send1.at[j], recv_sem=recv1.at[j],
-            device_id=nxt, device_id_type=MESH,
+        return pieces(src, h1.at[j], send1.at[j], recv1.at[j])
+
+    def copy2(j, src):
+        return pieces(src, w2.at[j], send2.at[j], recv2.at[j])
+
+    def start(copies):
+        for copy in copies:
+            copy.start()
+
+    def wait_send(copies):
+        for copy in copies:
+            copy.wait_send()
+
+    def wait_recv(copies):
+        for copy in copies:
+            copy.wait_recv()
+
+    def load(j):
+        others = (pl.ds(0, reach), pl.ds(reach + 1, reach))
+        return [
+            pltpu.make_async_copy(blocks.at[j, cut], blk.at[j, cut], load_sem.at[j, n])
+            for n, cut in enumerate(others)
+        ]
+
+    def load_diagonal(j):
+        return pltpu.make_async_copy(
+            blocks.at[j, reach], blk.at[j, reach], load_sem.at[j, 2]
         )
-
-    def copy2(j, src):
-        return pltpu.make_async_remote_copy(
-            src_ref=src, dst_ref=w2.at[j], send_sem=send2.at[j], recv_sem=recv2.at[j],
-            device_id=nxt, device_id_type=MESH,
-        )
-
-    def load(j):
-        return pltpu.make_async_copy(blocks.at[j], blk.at[j], load_sem.at[j])
 
     def raw_upper(j):
         return blocks.at[j, pl.ds(reach, reach + 1)]
 
-    aux_head = aux.at[:, pl.ds(0, SENT)]
+    aux_head = aux_own.at[:, pl.ds(0, SENT)]
     to_next = pltpu.make_async_remote_copy(
         src_ref=aux_head, dst_ref=aux_prev, send_sem=aux_send.at[0], recv_sem=aux_recv.at[0],
         device_id=nxt, device_id_type=MESH,
@@ -70,11 +88,13 @@
         src_ref=aux_head, dst_ref=aux_next, send_sem=aux_send.at[1], recv_sem=aux_recv.at[1],
         device_id=prv, device_id_type=MESH,
     )
-    aux_load = pltpu.make_async_copy(aux, aux_own, aux_load_sem.at[0])
-
-    aux_load.start()
+    shift_load = pltpu.make_async_copy(shifts, shift_own, aux_load_sem.at[0])
+
+    shift_load.start()
     for j in range(rows):
-        load(j).start()
+        load_diagonal(j).start()
+    for j in range(rows):
+        start(load(j))
 
     barrier = pltpu.get_barrier_semaphore()
 
@@ -88,18 +108,10 @@
 
     pl.semaphore_wait(barrier, has_prev.astype(jnp.int32) + has_next.astype(jnp.int32))
 
-    @pl.when(has_prev)
-    def _():
-        to_prev.start()
-
-    @pl.when(has_next)
-    def _():
-        to_next.start()
-
     @pl.when(inner)
     def _():
         for j in reversed(range(rows)):
-            copy1(j, raw_upper(j)).start()
+            start(copy1(j, raw_upper(j)))
 
     row_id = lax.broadcasted_iota(jnp.int32, (size, size), 0)
     col_id = lax.broadcasted_iota(jnp.int32, (size, size), 1)
@@ -124,7 +136,35 @@
     def _():
         aux_next[...] = jnp.zeros_like(aux_next)
 
-    aux_load.wait()
+    shift_load.wait()
+    for j in range(rows):
+        load_diagonal(j).wait()
+        diagonal = jnp.sum(
+            jnp.where(eye, blk[j, reach].astype(F32), 0.0), axis=0, keepdims=True
+        )
+        aux_own[j, DIAG : DIAG + 1, :] = shift_own[j] + diagonal
+        aux_own[j, SHIFT : SHIFT + 1, :] = shift_own[j]
+        row = here * rows + j
+        for k in range(band):
+            away = abs(k - reach)
+            if k < reach:
+                count = jnp.where(row - away >= 0, offsets[j, 0], 0)
+            else:
+                count = jnp.where(row + away < slabs * groups * rows, offsets[j, 1], 0)
+            marks = jnp.where(jnp.full((1, size), count, jnp.int32) >= away, 1.0, 0.0)
+            place = UPPER + k - reach if k >= reach else LOWER + k
+            aux_own[j, place : place + 1, :] = marks
+        if UPPER + reach + 1 < LOWER:
+            spare = LOWER - UPPER - reach - 1
+            aux_own[j, UPPER + reach + 1 : LOWER, :] = jnp.zeros((spare, size), F32)
+
+    @pl.when(has_next)
+    def _():
+        to_next.start()
+
+    @pl.when(has_prev)
+    def _():
+        to_prev.start()
 
     @pl.when(has_prev)
     def _():
@@ -151,7 +191,8 @@
         return jnp.where(mask_of(table, j, k), value, 0.0).astype(BF16)
 
     def scale_own(j, carry):
-        load(j).wait()
+        for copy in load(j):
+            copy.wait()
         left = as_column(scale[rows + j])
         shift = aux_own[j, SHIFT : SHIFT + 1, :]
         for k in range(band):
@@ -201,7 +242,7 @@
 
         @pl.when(has_prev)
         def _():
-            copy1(j, w2.at[reach + j]).wait_recv()
+            wait_recv(copy1(j, w2.at[reach + j]))
 
         @pl.when(grp > 0)
         def _():
@@ -227,11 +268,11 @@
 
         @pl.when(inner)
         def _():
-            copy2(j, w2.at[reach + j]).start()
+            start(copy2(j, w2.at[reach + j]))
 
         @pl.when(edge)
         def _():
-            copy1(j, w2.at[reach + j]).start()
+            start(copy1(j, w2.at[reach + j]))
 
         return carry
 
@@ -242,7 +283,7 @@
 
         @pl.when(has_prev)
         def _():
-            copy2(j, w2.at[reach + j]).wait_recv()
+            wait_recv(copy2(j, w2.at[reach + j]))
 
         def put(k, value):
             f2[j, k] = value
@@ -251,22 +292,18 @@
 
         @pl.when(edge)
         def _():
-            copy2(j, f2.at[j, pl.ds(reach, reach + 1)]).start()
-
-        pltpu.make_async_copy(f2.at[j], out.at[j], out_sem.at[j]).start()
+            start(copy2(j, f2.at[j, pl.ds(reach, reach + 1)]))
+
         return carry
 
     lax.fori_loop(0, rows, second_sweep, 0)
-
-    for j in range(rows):
-        pltpu.make_async_copy(f2.at[j], out.at[j], out_sem.at[j]).wait()
 
     @pl.when(has_next)
     def _():
         to_next.wait_send()
         for j in range(rows):
-            copy1(j, w2.at[reach + j]).wait_send()
-            copy2(j, w2.at[reach + j]).wait_send()
+            wait_send(copy1(j, w2.at[reach + j]))
+            wait_send(copy2(j, w2.at[reach + j]))
 
     @pl.when(has_prev)
     def _():
@@ -278,31 +315,23 @@
     reach = (band - 1) // 2
     assert rows == reach and reach <= 4
     slabs, groups = lax.axis_size("slab"), lax.axis_size("grp")
-    first_row = (lax.axis_index("slab") * groups + lax.axis_index("grp")) * rows
-    shift = diag_shift.reshape(rows, size)
-    eye = jnp.eye(size, dtype=bool)
-    diagonal = jnp.sum(jnp.where(eye[None], blocks[:, reach].astype(F32), 0.0), axis=1)
-    present = band_pattern(
-        first_row + jnp.arange(rows, dtype=jnp.int32), offsets, band, rows * slabs * groups
-    ).astype(F32)
-    marks = jnp.broadcast_to(present[:, :, None], (rows, band, size))
-    pieces = [(shift + diagonal)[:, None], shift[:, None], marks[:, reach:]]
-    pieces.append(jnp.zeros((rows, LOWER - UPPER - reach - 1, size), F32))
-    pieces.append(marks[:, :reach])
-    pieces.append(jnp.zeros((rows, 16 - LOWER - reach, size), F32))
-    aux = jnp.concatenate(pieces, axis=1)
-
+    shift = diag_shift.reshape(rows, 1, size)
     block = (size, size)
     upper = (reach + 1,) + block
     dma = pltpu.SemaphoreType.DMA
     return pl.pallas_call(
         functools.partial(kernel, slabs, groups, reach),
-        out_shape=jax.ShapeDtypeStruct(blocks.shape, BF16),
-        in_specs=[pl.BlockSpec(memory_space=pl.ANY)] * 2,
-        out_specs=pl.BlockSpec(memory_space=pl.ANY),
+        out_shape=pltpu.VMEM(blocks.shape, BF16),
+        in_specs=[
+            pl.BlockSpec(memory_space=pltpu.HBM),
+            pl.BlockSpec(memory_space=pltpu.HBM),
+            pl.BlockSpec(memory_space=pltpu.SMEM),
+        ],
+        out_specs=pl.BlockSpec(memory_space=pltpu.VMEM),
         scratch_shapes=[
             pltpu.VMEM(blocks.shape, BF16),
-            pltpu.VMEM(aux.shape, F32),
+            pltpu.VMEM((rows, 1, size), F32),
+            pltpu.VMEM((rows, 2 * SENT, size), F32),
             pltpu.VMEM((rows, SENT, size), F32),
             pltpu.VMEM((rows, SENT, size), F32),
             pltpu.VMEM((3 * rows, 1, size), F32),
@@ -311,12 +340,11 @@
             pltpu.VMEM((reach + rows,) + upper, BF16),
             pltpu.VMEM((rows, reach) + block, BF16),
             pltpu.VMEM((rows,) + upper, BF16),
-            pltpu.VMEM(blocks.shape, BF16),
-            dma((rows,)), dma((1,)), dma((rows,)), dma((2,)), dma((2,)),
-            dma((rows,)), dma((rows,)), dma((rows,)), dma((rows,)),
+            dma((rows, 3)), dma((1,)), dma((2,)), dma((2,)),
+            dma((rows, 3)), dma((rows, 3)), dma((rows, 3)), dma((rows, 3)),
         ],
-        compiler_params=pltpu.CompilerParams(collective_id=0, has_side_effects=True),
-    )(blocks, aux)
+        compiler_params=pltpu.CompilerParams(collective_id=0, has_side_effects=True, vmem_limit_bytes=57 << 20),
+    )(blocks, shift, offsets)
 
 
 def solution(mesh):

time: 84.6 us -> 95.3 us (1.13)
  the two profiles are of different devices: /device:TPU:2 before, /device:TPU:14 now
where the time goes in v1:
time: 95.3 us; the launch traced here: 95.1 us
  Pallas kernels  91.6 us (96%)
  local copies, waits for them, and re-layouts  3.52 us (4%)
    pallas_call x1, Pallas kernels, per_device(): pl.pallas_call(functools.partial(kernel, slabs, groups, reach), out_shape...  91.6 us
    unnamed x2, local copies, waits for them, and re-layouts  3.52 us

profile of v1, /device:TPU:14, one launch (start us, length us, event | category | flops | bytes accessed | tf_op | source)
XLA Modules:
  0.0 95.1 jit_solution(8157668324098707042)
XLA Ops:
  0.0 1.3 %copy.4.offsets = s32[4,2]{1,0:T(4,128)} copy(s32[4,2]{0,1:T(2,128)} %param.5) | data formatting | bytes 64 | tf_op args[2]
  1.3 91.6 %shard_map.37 = bf16[4,9,256,256]{3,2,1,0:T(8,128)(2,1)S(1)} custom-call(bf16[4,9,256,256]{3,2,1,0:T(8,128)(2,1)} %blocks.1, f32[4,1,256]{2,1,0:T(1,128)} %bitcast.1, s32[4,2]{1,0:T(4,128)} %copy.4.offsets), custom_call_target="tpu_custom_call" | custom-call | tf_op jit(solution)/shard_map/pallas_call | solution.py:322
  92.9 2.2 %copy.6 = bf16[4,9,256,256]{3,2,1,0:T(8,128)(2,1)} copy(bf16[4,9,256,256]{3,2,1,0:T(8,128)(2,1)S(1)} %shard_map.37) | data formatting | bytes 9437184
